TPU v7x, 256 devices: a whole 4x4x8 slice. The times are simulated.
256 devices in a mesh: slab: 32 (over z, y), energy: 8 (over x, core).
Axes of the slice: x: 4, y: 4, z: 8, core: 2. Of those that a mesh axis runs over, the one named last changes fastest.
Arguments:
- green: bfloat16 [8, 32, 3, 2, 384, 384], P('energy', 'slab'), may hold values from -0.3125 to 0.3125
- sigma: bfloat16 [8, 32, 3, 2, 384, 384], P('energy', 'slab'), may hold values from -4 to 4
- phonon: bfloat16 [8, 32, 2, 384, 384], P('energy', 'slab'), may hold values from -4 to 4
- pair_off: int32 [32, 3], replicated, may hold values from -2 to 2, as said below
- pair_count: int32 [32], replicated, may hold values from 1 to 3, as said below
- pair_range: int32 [32, 3], replicated, may hold values from 96 to 384, as said below
Outputs:
- lesser: float32 [8, 32, 2, 384, 384], P('energy', 'slab')
Inputs may be any that keep to these rules, and one draw needn't show every extreme that they name: The partner slab k + pair_off[k, q] lies inside the grid. `pair_count`: some slab has 3 live slots. `pair_range`: a multiple of 96; some pair couples all 384 orbitals.
All inputs are finite; a program needn't handle non-finite values.
Results may differ from a plain program's by a relative error of at most 0.0035.
Values may be sent and summed in bfloat16 or wider, within the bound.
No kernel may reach another device: no remote copies, remote signals or barrier semaphores. Data moves between devices by JAX's collectives and lax.ppermute only.
A program may use at most 64 MiB of HBM per device.

v0:
```python
import functools

import jax
import jax.numpy as jnp
from jax import lax
from jax.experimental import pallas as pl
from jax.experimental.pallas import tpu as pltpu
from jax.sharding import PartitionSpec as P


F32 = jnp.float32
BF16 = jnp.bfloat16
VMEM_LIMIT = 24 * 1024 * 1024
CHUNKS = 3
PIECE = 16
STRIP = 96
LEVELS = (192, 288, 384)
SPLIT = 256


def cost(flops, moved):
    return pl.CostEstimate(flops=int(flops), bytes_accessed=int(moved), transcendentals=0)


def dot(left, right):
    return jnp.dot(left, right, preferred_element_type=F32)


def toward():
    return 1 - 2 * lax.rem(lax.axis_index("slab"), 2)


def matches(slab, offset, off, cnt, rng):
    found = []
    for q in range(off.shape[0]):
        live = (off[q, slab] == offset) & (q < cnt[slab])
        found.append((live.astype(jnp.int32), jnp.where(live, rng[q, slab], 0)))
    return found


def inside(lanes, reach, first):
    return (lanes < jnp.where(first < reach, reach, 0)).astype(F32).astype(BF16)


def strip_sum(sigma, part, reaches, lanes, c):
    slots, _, height, width = sigma.shape
    total = jnp.zeros((height, width), F32)
    for q in range(slots):
        total = total + (sigma[q, part] * inside(lanes, reaches[q], c * height)).astype(F32)
    return total


def packing(reach, width):
    if reach == width:
        return 2 * width, width, 0
    body = reach // 128 * 128
    rest = reach - body
    units = (2 * body // 128 + 1) * (reach // PIECE)
    if folded(rest):
        units -= reach // PIECE // 2
    lanes = 2 * width // 128
    return width + -(-units // lanes) * PIECE, body, rest


def folded(rest):
    return 4 * rest <= 128


def unit_at(group, piece, reach, width):
    lanes = 2 * width // 128
    unit = group * (reach // PIECE) + piece
    row, lane = width + unit // lanes * PIECE, unit % lanes * 128
    return slice(row, row + PIECE), slice(lane, lane + 128)


def widest_small(off, cnt, rng):
    slots = lax.broadcasted_iota(jnp.int32, off.shape, 0)
    live = slots < cnt[...]

    def reach(offset):
        return jnp.max(jnp.where(live & (off[...] == offset), rng[...], 0), axis=0, keepdims=True)

    low = jnp.minimum(reach(-1), reach(-2))
    high = jnp.minimum(reach(1), reach(2))
    return jnp.max(jnp.maximum(low, high))


def near_leads(slab, d, off, cnt, rng):
    near, far = [
        functools.reduce(jnp.maximum, [reach for _, reach in matches(slab, offset, off, cnt, rng)])
        for offset in (d, 2 * d)
    ]
    return near >= far


def side_kernel(off_in, cnt_in, rng_in, sigma, *refs):
    outs, (level, roles) = refs[: 2 * len(LEVELS)], refs[2 * len(LEVELS) : 2 * len(LEVELS) + 2]
    off, cnt, rng, off_v, cnt_v, rng_v, held, sems, table_sems = refs[2 * len(LEVELS) + 2 :]
    slab = lax.axis_index("slab")
    s = toward()
    chunks, slots, _, height, width = held.shape
    moves = (
        (off_in, off_v),
        (cnt_in, cnt_v),
        (rng_in, rng_v),
        (off_in, off),
        (cnt_in, cnt),
        (rng_in, rng),
    )
    tables = [
        pltpu.make_async_copy(src, dst, table_sems.at[n]) for n, (src, dst) in enumerate(moves)
    ]
    copies = [
        pltpu.make_async_copy(
            sigma.at[0, 0, :, :, pl.ds(c * height, height), :], held.at[c], sems.at[c]
        )
        for c in range(chunks)
    ]
    for copy in tables + copies:
        copy.start()
    for copy in tables:
        copy.wait()
    widest = widest_small(off_v, cnt_v, rng_v)
    rank = sum((widest > reach).astype(jnp.int32) for reach in LEVELS[:-1])
    level[0] = rank
    cnt = cnt.at[0]
    last = off.shape[1] - 1
    for n, d in enumerate((s, -s)):
        neighbour = jnp.clip(slab + d, 0, last)
        roles[n] = near_leads(neighbour, -d, off, cnt, rng).astype(jnp.int32)

    merges, messages = [], []
    for d in (s, -s):
        sides = []
        for offset in (d, 2 * d):
            found = matches(slab, offset, off, cnt, rng)
            number = sum(live for live, _ in found)
            which = jnp.int32(0)
            for q in reversed(range(slots)):
                which = jnp.where(found[q][0] > 0, q, which)
            reach = functools.reduce(jnp.maximum, [reach for _, reach in found])
            merges.append((number, which, [reach for _, reach in found]))
            sides.append((which, reach))
        near, far = sides
        leads = near[1] >= far[1]
        big = tuple(jnp.where(leads, u, v) for u, v in zip(near, far))
        small = tuple(jnp.where(leads, v, u) for u, v in zip(near, far))
        messages.append((big, small))

    lanes = lax.broadcasted_iota(jnp.int32, (1, width), 1)
    shared = functools.reduce(jnp.maximum, [number for number, _, _ in merges]) > 1

    @pl.when(shared)
    def _():
        for c in range(chunks):
            copies[c].wait()
            for number, which, reaches in merges:

                @pl.when(number > 1)
                def _():
                    for part in range(2):
                        total = strip_sum(held.at[c], part, reaches, lanes, c)
                        held[c, which, part] = total.astype(BF16)

    for index, reach in enumerate(LEVELS):

        @pl.when(rank == index)
        def _():
            for c in range(chunks):
                pl.when(jnp.logical_not(shared))(copies[c].wait)
                for n, message in enumerate(messages):
                    write_strip(outs[2 * index + n], held.at[c], message, reach, lanes, c)


def write_strip(out, held, message, reach, lanes, c):
    big, small = message
    _, _, height, width = held.shape
    keep_big = inside(lanes, big[1], c * height)
    keep_small = inside(lanes, small[1], c * height)
    whole = [slice(part * width, (part + 1) * width) for part in range(2)]
    for part in range(2):
        out[c * height : (c + 1) * height, whole[part]] = held[big[0], part] * keep_big
    _, body, rest = packing(reach, width)
    if rest == 0:
        for part in range(2):
            first = width + c * height
            out[first : first + height, whole[part]] = held[small[0], part] * keep_small
        return
    if c * height >= reach:
        return
    parts = [
        held[small[0], part, :, : body + 128] * keep_small[:, : body + 128] for part in range(2)
    ]
    tail = parts[0][:, body:].astype(F32) + pltpu.roll(parts[1][:, body:].astype(F32), rest, 1)
    units = [part[:, at : at + 128] for part in parts for at in range(0, body, 128)]
    half = reach // PIECE // 2
    for n in range(height // PIECE):
        piece = c * height // PIECE + n
        rows = slice(n * PIECE, (n + 1) * PIECE)
        for group, unit in enumerate(units):
            out[unit_at(group, piece, reach, width)] = unit[rows]
        if folded(rest) and piece >= half:
            at = unit_at(len(units), piece - half, reach, width)
            out[at] = out[at] + pltpu.roll(tail[rows], 64, 1).astype(BF16)
        else:
            out[unit_at(len(units), piece, reach, width)] = tail[rows].astype(BF16)


def own_kernel(off, cnt, rng, sigma, near_first, near_second, middle):
    slab = lax.axis_index("slab")
    cnt = cnt.at[0]
    _, _, _, width = sigma.shape[2:]
    lanes = lax.broadcasted_iota(jnp.int32, (1, width), 1)
    c = pl.program_id(0)
    for offset, out in ((toward(), near_first), (-toward(), near_second), (0, middle)):
        reaches = [reach for _, reach in matches(slab, offset, off, cnt, rng)]
        for part in range(2):
            total = strip_sum(sigma.at[0, 0], part, reaches, lanes, c)
            out[:, part * width : (part + 1) * width] = total.astype(out.dtype)


def centre_kernel(middle, one, two, early, late):
    width = middle.shape[1] // 2
    for part in range(2):
        mixed = 0.5 * (one[0, 0, part].astype(F32) + two[0, 0, part].astype(F32))
        at = slice(part * width, (part + 1) * width)
        total = (middle[:, at] + mixed.astype(BF16).astype(F32)).astype(BF16)
        early[:, at] = total[:SPLIT]
        late[:, at] = total[SPLIT:]


def green_kernel(green, right, left, left_early, left_late):
    width = green.shape[-1]
    s = toward()
    for slot, o in enumerate((1 + s, 1, 1 - s)):
        real, imag = green[0, 0, o, 0], green[0, 0, o, 1]
        real_t, imag_t = real.T, imag.T
        at = 2 * slot * width
        right[at : at + width, :width] = real_t
        right[at : at + width, width:] = -imag_t
        right[at + width : at + 2 * width, :width] = imag_t
        right[at + width : at + 2 * width, width:] = real_t
        if slot == 1:
            left[:, :width] = real
            left[:, width:] = imag
        else:
            for out, first, last in ((left_early, 0, SPLIT), (left_late, SPLIT, width)):
                height = last - first
                to = slot * height
                out[:, to : to + height] = real[:, first:last]
                out[:, to + height : to + 2 * height] = imag[:, first:last]


def spread(x, out, first):
    height, width = x.shape[0], x.shape[1] // 2
    rounded = x.astype(BF16)
    real, imag = rounded[:, :width], rounded[:, width:]
    out[first : first + height, :width] = real
    out[first : first + height, width:] = imag
    out[first + height : first + 2 * height, :width] = -imag
    out[first + height : first + 2 * height, width:] = real


def local_kernel(near_first, early, late, near_second, right, left, out, held):
    wide = early.shape[1]
    x = dot(near_first[...], right[:wide]) + dot(near_second[...], right[2 * wide :])
    middle = right[wide : 2 * wide]
    x = x + jnp.concatenate([dot(early[...], middle), dot(late[...], middle)], axis=0)
    spread(x, held, 0)
    out[...] = dot(left[...], held[...])


def arrive_kernel(reach, roles, from_first, from_second, right, out_first, out_second, *packed):
    width, wide = out_first.shape
    for n, (message, out, other) in enumerate(
        ((from_first, out_first, 2 * wide), (from_second, out_second, 0))
    ):
        leads = roles[n] > 0
        big_at = pl.multiple_of(jnp.where(leads, wide, other), wide)
        small_at = pl.multiple_of(jnp.where(leads, other, wide), wide)
        total = dot(message[:width], right[pl.ds(big_at, wide)])
        if reach == width:
            out[...] = total + dot(message[width:], right[pl.ds(small_at, wide)])
            continue
        left, down = packed
        _, body, rest = packing(reach, width)
        groups, pieces = 2 * body // 128, reach // PIECE
        for group in range(groups):
            for piece in range(pieces):
                left[piece * PIECE : (piece + 1) * PIECE, group * 128 : (group + 1) * 128] = (
                    message[unit_at(group, piece, reach, width)]
                )
        tails = pieces // 2 if folded(rest) else pieces
        for piece in range(tails):
            left[piece * PIECE : (piece + 1) * PIECE, 2 * body :] = (
                message[unit_at(groups, piece, reach, width)]
            )
        for part in range(2):
            source = pl.multiple_of(small_at + part * width, width)
            down[part * body : (part + 1) * body] = right[pl.ds(source, body)]
            tail = pl.multiple_of(small_at + part * width + body, 128)
            to = 2 * body + part * rest
            down[to : to + rest] = right[pl.ds(tail, rest)]
        if not folded(rest):
            out[:reach] = total[:reach] + dot(left[...], down[: 2 * body + 128])
            out[reach:] = total[reach:]
            continue
        first, last, half = 2 * body, 2 * body + 128, reach // 2
        down[first + 64 : last] = jnp.zeros((64, wide), BF16)
        down[last : last + 64] = jnp.zeros((64, wide), BF16)
        down[last + 64 : last + 128] = down[first : first + 64]
        ends = left[:half, first:last]
        total_small = dot(left[:, :first], down[:first])
        out[:half] = total[:half] + total_small[:half] + dot(ends, down[first:last])
        out[half:reach] = total[half:reach] + total_small[half:] + dot(ends, down[last : last + 128])
        out[reach:] = total[reach:]


def fold(c_first, c_second, x_first, x_second, right, held, first):
    height, wide = c_first.shape
    top = slice(first, first + height)
    spread(x_first[top, :] + dot(c_first[...], right[:wide]), held, 0)
    spread(x_second[top, :] + dot(c_second[...], right[2 * wide :]), held, 2 * height)


def early_kernel(c_first, c_second, x_first, x_second, right, left, partial, out, held):
    fold(c_first, c_second, x_first, x_second, right, held, 0)
    out[...] = partial[...] + dot(left[...], held[...])


def late_kernel(c_first, c_second, x_first, x_second, right, left, partial, out, held, stage, sems):
    width = stage.shape[-1]
    fold(c_first, c_second, x_first, x_second, right, held, SPLIT)
    height = width // CHUNKS
    copies = []
    for c in range(CHUNKS):
        top = pl.ds(c * height, height)
        total = partial[top, :] + dot(left[top, :], held[...])
        stage[0, top, :] = total[:, :width]
        stage[1, top, :] = total[:, width:]
        copies.append(
            pltpu.make_async_copy(stage.at[:, top, :], out.at[0, 0, :, top, :], sems.at[c])
        )
        copies[-1].start()
    for copy in copies:
        copy.wait()


def smem():
    return pl.BlockSpec(memory_space=pltpu.SMEM)


def hbm():
    return pl.BlockSpec(memory_space=pltpu.HBM)


def params():
    return pltpu.CompilerParams(vmem_limit_bytes=VMEM_LIMIT)


def swaps(first, count):
    pairs = []
    for i in range(first, count - 1, 2):
        pairs += [(i, i + 1), (i + 1, i)]
    return pairs


def swap(value, axis, first):
    return lax.ppermute(value, axis, swaps(first, lax.axis_size(axis)))


def in_hbm(value):
    return pltpu.with_memory_space_constraint(value, pltpu.HBM)


def program(green, sigma, phonon, pair_off, pair_count, pair_range):
    width = green.shape[-1]
    wide = 2 * width
    slots = sigma.shape[2]
    tables = (pair_off.T, pair_count[None], pair_range.T)
    block_bytes = 2 * width * wide
    chunks = width // STRIP

    messages = []
    for reach in LEVELS:
        rows = packing(reach, width)[0]
        messages += [jax.ShapeDtypeStruct((rows, wide), BF16)] * 2
    *messages, level, roles = pl.pallas_call(
        side_kernel,
        in_specs=[hbm()] * 4,
        out_specs=[pl.BlockSpec(memory_space=pltpu.VMEM)] * len(messages) + [smem(), smem()],
        out_shape=[
            *messages,
            pltpu.SMEM((1,), jnp.int32),
            pltpu.SMEM((2,), jnp.int32),
        ],
        scratch_shapes=[
            *[pltpu.SMEM(table.shape, jnp.int32) for table in tables],
            *[pltpu.VMEM(table.shape, jnp.int32) for table in tables],
            pltpu.VMEM((chunks, slots, 2, STRIP, width), BF16),
            pltpu.SemaphoreType.DMA((chunks,)),
            pltpu.SemaphoreType.DMA((6,)),
        ],
        compiler_params=params(),
        cost_estimate=cost(3e9, 7 * block_bytes),
        name="side",
    )(*[in_hbm(value) for value in (*tables, sigma)])
    branches = [functools.partial(remainder, reach, 2 * n) for n, reach in enumerate(LEVELS)]
    return lax.switch(level[0], branches, messages, roles, green, sigma, phonon, tables)


def remainder(reach, index, messages, roles, green, sigma, phonon, tables):
    first, second = messages[index : index + 2]
    width = green.shape[-1]
    wide = 2 * width
    slots = sigma.shape[2]
    block_bytes = 2 * width * wide
    from_first = swap(first, "slab", 0)
    from_second = swap(second, "slab", 1)

    one = swap(phonon, "energy", 0)
    two = swap(phonon, "energy", 1)

    tall = pl.BlockSpec((STRIP, wide), lambda c: (c, 0))
    near_first, near_second, middle = pl.pallas_call(
        own_kernel,
        grid=(width // STRIP,),
        in_specs=[
            *[smem()] * 3,
            pl.BlockSpec((1, 1, slots, 2, STRIP, width), lambda c: (0, 0, 0, 0, c, 0)),
        ],
        out_specs=[tall] * 3,
        out_shape=[
            jax.ShapeDtypeStruct((width, wide), BF16),
            jax.ShapeDtypeStruct((width, wide), BF16),
            jax.ShapeDtypeStruct((width, wide), F32),
        ],
        compiler_params=params(),
        cost_estimate=cost(3e9, 7 * block_bytes),
        name="own",
    )(*[in_hbm(value) for value in (*tables, sigma)])

    early, late = pl.pallas_call(
        centre_kernel,
        out_shape=[
            jax.ShapeDtypeStruct((SPLIT, wide), BF16),
            jax.ShapeDtypeStruct((width - SPLIT, wide), BF16),
        ],
        compiler_params=params(),
        cost_estimate=cost(1e9, 5 * block_bytes),
        name="centre",
    )(middle, one, two)
    early_second = swap(early, "slab", 1)
    early_first = swap(early, "slab", 0)
    late_second = swap(late, "slab", 1)
    late_first = swap(late, "slab", 0)

    right, left, left_early, left_late = pl.pallas_call(
        green_kernel,
        out_shape=[
            jax.ShapeDtypeStruct((3 * wide, wide), BF16),
            jax.ShapeDtypeStruct((width, wide), BF16),
            jax.ShapeDtypeStruct((width, 4 * SPLIT), BF16),
            jax.ShapeDtypeStruct((width, 4 * (width - SPLIT)), BF16),
        ],
        compiler_params=params(),
        cost_estimate=cost(4e9, 12 * block_bytes),
        name="green",
    )(in_hbm(green))

    square = jax.ShapeDtypeStruct((width, wide), F32)
    unit = 2 * width * wide * wide
    partial = pl.pallas_call(
        local_kernel,
        out_shape=square,
        scratch_shapes=[pltpu.VMEM((wide, wide), BF16)],
        compiler_params=params(),
        cost_estimate=cost(4 * unit, 16 * block_bytes),
        name="local",
    )(near_first, early, late, near_second, right, left)

    _, body, rest = packing(reach, width)
    depth = 2 * body + 128
    packed = [pltpu.VMEM((reach, depth), BF16), pltpu.VMEM((depth + 128, wide), BF16)]
    x_first, x_second = pl.pallas_call(
        functools.partial(arrive_kernel, reach),
        in_specs=[smem()] + [pl.BlockSpec(memory_space=pltpu.VMEM)] * 3,
        out_shape=[square, square],
        scratch_shapes=packed if rest else [],
        compiler_params=params(),
        cost_estimate=cost(4 * unit, 16 * block_bytes),
        name="arrive",
    )(roles, from_first, from_second, right)

    partial = pl.pallas_call(
        early_kernel,
        out_shape=square,
        scratch_shapes=[pltpu.VMEM((4 * SPLIT, wide), BF16)],
        compiler_params=params(),
        cost_estimate=cost(3 * unit, 16 * block_bytes),
        name="early",
    )(early_first, early_second, x_first, x_second, right, left_early, partial)

    return pl.pallas_call(
        late_kernel,
        out_specs=hbm(),
        out_shape=pltpu.HBM((1, 1, 2, width, width), F32),
        scratch_shapes=[
            pltpu.VMEM((4 * (width - SPLIT), wide), BF16),
            pltpu.VMEM((2, width, width), F32),
            pltpu.SemaphoreType.DMA((CHUNKS,)),
        ],
        compiler_params=params(),
        cost_estimate=cost(2 * unit, 16 * block_bytes),
        name="late",
    )(late_first, late_second, x_first, x_second, right, left_late, partial)


def solution(mesh):
    in_specs = (
        P("energy", "slab", None, None, None, None),
        P("energy", "slab", None, None, None, None),
        P("energy", "slab", None, None, None),
        P(),
        P(),
        P(),
    )
    out_specs = P("energy", "slab", None, None, None)
    return jax.shard_map(program, mesh=mesh, in_specs=in_specs, out_specs=out_specs, check_vma=False)
```

profile of v0, /device:TPU:130, one launch (start us, length us, event | category | flops | bytes accessed | tf_op | source)
XLA Modules:
  0.0 49.8 jit_solution(8322148598261229539)
XLA Ops:
  0.0 0.0 copy-start
  0.0 2.6 %side.1 = (bf16[480,768]{1,0:T(8,128)(2,1)S(1)}, bf16[480,768]{1,0:T(8,128)(2,1)S(1)}, bf16[608,768]{1,0:T(8,128)(2,1)S(1)}, bf16[608,768]{1,0:T(8,128)(2,1)S(1)...) custom-call(s32[3,32]{1,0:T(4,128)} %bitcast.4, ...), custom_call_target="tpu_custom_call" | custom-call | flops 3000000000 | bytes 4128768 | tf_op jit(solution)/shard_map/side/pallas_call | solution.py:388
  2.6 0.0 copy-done
  2.7 46.9 %conditional.1 = (f32[1,1,2,384,384]{4,3,2,1,0:T(8,128)}) conditional(s32[]{:T(128)} %bitcast.3, (s32[3,32]{1,0:T(4,128)}, s32[1,32]{1,0:T(1,128)}, s32[3,32]{1,0:T(4,128)}, bf16[1,1,3,2,384,384]{5,4,3,2,1,0:T(8,128)(2,1)}, bf16[1,1,2,384,384]{4,3,2,1,0:T(8,128)(2,1)S(1)}, /*index=5*/bf16[480,768]{1,0:T(8,128)(2,1)S(1)}, ...), branch_computations={%region_0.0_spmd, %region_1.0_spmd, %region_2.0_spmd} | conditional | flops 13888802816 | bytes 70779208 | solution.py:409
  2.9 0.1 collective-permute-start.8
  3.0 2.5 %collective-permute-start.9 = (bf16[1,1,2,384,384]{4,3,2,1,0:T(8,128)(2,1)S(1)}, bf16[1,1,2,384,384]{4,3,2,1,0:T(8,128)(2,1)S(1)}, u32[]{:S(2)}, u32[]{:S(2)}) collective-permute-start(bf16[1,1,2,384,384]{4,3,2,1,0:T(8,128)(2,1)S(1)} %get-tuple-element.88), channel_id=1, source_target_pairs={{1,2},{2,1},{3,4},{4,3},{5,6},{6,5},{9,10},{10,9},{11,12},{12,11},... | collective-permute-start | bytes 1769480 | tf_op jit(solution)/shard_map/cond/branch_1_fun/ppermute | solution.py:369
  5.5 0.8 %collective-permute-start.12 = (bf16[608,768]{1,0:T(8,128)(2,1)S(1)}, bf16[608,768]{1,0:T(8,128)(2,1)S(1)}, u32[]{:S(2)}, u32[]{:S(2)}) collective-permute-start(bf16[608,768]{1,0:T(8,128)(2,1)S(1)} %get-tuple-element.91), channel_id=1, source_target_pairs={{0,8},{8,0},{16,24},{24,16},{32,40},{40,32},{48,56},{56,48},{64,72... | collective-permute-start | bytes 2801672 | tf_op jit(solution)/shard_map/cond/branch_1_fun/ppermute | solution.py:369
  6.4 3.6 %collective-permute-start.13 = (bf16[608,768]{1,0:T(8,128)(2,1)S(1)}, bf16[608,768]{1,0:T(8,128)(2,1)S(1)}, u32[]{:S(2)}, u32[]{:S(2)}) collective-permute-start(bf16[608,768]{1,0:T(8,128)(2,1)S(1)} %get-tuple-element.92), channel_id=1, source_target_pairs={{8,16},{16,8},{24,32},{32,24},{40,48},{48,40},{56,64},{64,56},{72,... | collective-permute-start | bytes 2801672 | tf_op jit(solution)/shard_map/cond/branch_1_fun/ppermute | solution.py:369
  10.0 2.9 %own.4 = (bf16[384,768]{1,0:T(8,128)(2,1)S(1)}, bf16[384,768]{1,0:T(8,128)(2,1)S(1)}, f32[384,768]{1,0:T(8,128)S(1)}) custom-call(s32[3,32]{1,0:T(4,128)} %get-tuple-element.83.off, s32[1,32]{1,0:T(1,128)} %get-tuple-element.84.cnt, s32[3,32]{1,0:T(4,128)} %get-tuple-element.85.rng, bf16[1,1,3,2,384,384]{5,4,3,2,1,0:T(8,128)(2,1)} %get-tuple-element.86.sigma), custom_call_target="tpu_custom_call" | custom-call | flops 3000000000 | bytes 4128768 | tf_op jit(solution)/shard_map/cond/branch_1_fun/own/pallas_call | solution.py:425
  12.9 0.0 collective-permute-done.8.one
  12.9 1.3 %collective-permute-done.9.two = bf16[1,1,2,384,384]{4,3,2,1,0:T(8,128)(2,1)S(1)} collective-permute-done((bf16[1,1,2,384,384]{4,3,2,1,0:T(8,128)(2,1)S(1)}, bf16[1,1,2,384,384]{4,3,2,1,0:T(8,128)(2,1)S(1)}, u32[]{:S(2)}, u32[]{:S(2)}) %collective-permute-start.9) | collective-permute-done | bytes 589856 | tf_op jit(solution)/shard_map/cond/branch_1_fun/ppermute | solution.py:369
  14.2 0.3 centre.4
  14.5 0.8 %collective-permute-start.14 = (bf16[256,768]{1,0:T(8,128)(2,1)S(1)}, bf16[256,768]{1,0:T(8,128)(2,1)S(1)}, u32[]{:S(2)}, u32[]{:S(2)}) collective-permute-start(bf16[256,768]{1,0:T(8,128)(2,1)S(1)} %get-tuple-element.98.early), channel_id=1, source_target_pairs={{0,8},{8,0},{16,24},{24,16},{32,40},{40,32},{48,56},{56,48},{64,72... | collective-permute-start | bytes 1179656 | tf_op jit(solution)/shard_map/cond/branch_1_fun/ppermute | solution.py:369
  15.3 3.6 %collective-permute-start.15 = (bf16[256,768]{1,0:T(8,128)(2,1)S(1)}, bf16[256,768]{1,0:T(8,128)(2,1)S(1)}, u32[]{:S(2)}, u32[]{:S(2)}) collective-permute-start(bf16[256,768]{1,0:T(8,128)(2,1)S(1)} %get-tuple-element.98.early), channel_id=1, source_target_pairs={{8,16},{16,8},{24,32},{32,24},{40,48},{48,40},{56,64},{64,56},{72,... | collective-permute-start | bytes 1179656 | tf_op jit(solution)/shard_map/cond/branch_1_fun/ppermute | solution.py:369
  18.9 2.1 %green.4 = (bf16[2304,768]{1,0:T(8,128)(2,1)S(1)}, bf16[384,768]{1,0:T(8,128)(2,1)S(1)}, bf16[384,1024]{1,0:T(8,128)(2,1)S(1)}, bf16[384,512]{1,0:T(8,128)(2,1)S(1)}) custom-call(bf16[1,1,3,2,384,384]{5,4,3,2,1,0:T(8,128)(2,1)} %get-tuple-element.93.green), custom_call_target="tpu_custom_call" | custom-call | flops 4000000000 | bytes 7077888 | tf_op jit(solution)/shard_map/cond/branch_1_fun/green/pallas_call | solution.py:458
  21.1 1.2 %collective-permute-start.10 = (bf16[128,768]{1,0:T(8,128)(2,1)S(1)}, bf16[128,768]{1,0:T(8,128)(2,1)S(1)}, u32[]{:S(2)}, u32[]{:S(2)}) collective-permute-start(bf16[128,768]{1,0:T(8,128)(2,1)S(1)} %get-tuple-element.89.late), channel_id=1, source_target_pairs={{0,8},{8,0},{16,24},{24,16},{32,40},{40,32},{48,56},{56,48},{64,72... | collective-permute-start | bytes 589832 | tf_op jit(solution)/shard_map/cond/branch_1_fun/ppermute | solution.py:369
  22.3 2.8 %local.4.partial = f32[384,768]{1,0:T(8,128)S(1)} custom-call(bf16[384,768]{1,0:T(8,128)(2,1)S(1)} %get-tuple-element.100.near_first, bf16[256,768]{1,0:T(8,128)(2,1)S(1)} %get-tuple-element.98.early, bf16[128,768]{1,0:T(8,128)(2,1)S(1)} %get-tuple-element.89.late, bf16[384,768]{1,0:T(8,128)(2,1)S(1)} %get-tuple-element.101.near_second, ...), custom_call_target="tpu_custom_call" | custom-call | flops 1811939328 | bytes 9437184 | tf_op jit(solution)/shard_map/cond/branch_1_fun/local/pallas_call | solution.py:473
  25.1 4.1 %collective-permute-done.12.from_first = bf16[608,768]{1,0:T(8,128)(2,1)S(1)} collective-permute-done((bf16[608,768]{1,0:T(8,128)(2,1)S(1)}, bf16[608,768]{1,0:T(8,128)(2,1)S(1)}, u32[]{:S(2)}, u32[]{:S(2)}) %collective-permute-start.12) | collective-permute-done | bytes 933920 | tf_op jit(solution)/shard_map/cond/branch_1_fun/ppermute | solution.py:369
  29.2 3.6 %collective-permute-start.11 = (bf16[128,768]{1,0:T(8,128)(2,1)S(1)}, bf16[128,768]{1,0:T(8,128)(2,1)S(1)}, u32[]{:S(2)}, u32[]{:S(2)}) collective-permute-start(bf16[128,768]{1,0:T(8,128)(2,1)S(1)} %get-tuple-element.89.late), channel_id=1, source_target_pairs={{8,16},{16,8},{24,32},{32,24},{40,48},{48,40},{56,64},{64,56},{72,... | collective-permute-start | bytes 589832 | tf_op jit(solution)/shard_map/cond/branch_1_fun/ppermute | solution.py:369
  32.8 2.3 %collective-permute-done.13.from_second = bf16[608,768]{1,0:T(8,128)(2,1)S(1)} collective-permute-done((bf16[608,768]{1,0:T(8,128)(2,1)S(1)}, bf16[608,768]{1,0:T(8,128)(2,1)S(1)}, u32[]{:S(2)}, u32[]{:S(2)}) %collective-permute-start.13) | collective-permute-done | bytes 933920 | tf_op jit(solution)/shard_map/cond/branch_1_fun/ppermute | solution.py:369
  35.1 1.8 %arrive.4 = (f32[384,768]{1,0:T(8,128)S(1)}, f32[384,768]{1,0:T(8,128)S(1)}) custom-call(s32[2]{0:T(128)S(4)} %get-tuple-element.90.roles, bf16[608,768]{1,0:T(8,128)(2,1)S(1)} %collective-permute-done.12.from_first, bf16[608,768]{1,0:T(8,128)(2,1)S(1)} %collective-permute-done.13.from_second, bf16[2304,768]{1,0:T(8,128)(2,1)S(1)} %get-tuple-element.94.right), custom_call_target="tpu_custom_call" | custom-call | flops 1811939328 | bytes 9437184 | tf_op jit(solution)/shard_map/cond/branch_1_fun/arrive/pallas_call | solution.py:485
  37.0 0.7 %collective-permute-done.14.c_first = bf16[256,768]{1,0:T(8,128)(2,1)S(1)} collective-permute-done((bf16[256,768]{1,0:T(8,128)(2,1)S(1)}, bf16[256,768]{1,0:T(8,128)(2,1)S(1)}, u32[]{:S(2)}, u32[]{:S(2)}) %collective-permute-start.14) | collective-permute-done | bytes 393248 | tf_op jit(solution)/shard_map/cond/branch_1_fun/ppermute | solution.py:369
  37.6 5.9 %collective-permute-done.15.c_second = bf16[256,768]{1,0:T(8,128)(2,1)S(1)} collective-permute-done((bf16[256,768]{1,0:T(8,128)(2,1)S(1)}, bf16[256,768]{1,0:T(8,128)(2,1)S(1)}, u32[]{:S(2)}, u32[]{:S(2)}) %collective-permute-start.15) | collective-permute-done | bytes 393248 | tf_op jit(solution)/shard_map/cond/branch_1_fun/ppermute | solution.py:369
  43.6 1.4 %early.4.partial = f32[384,768]{1,0:T(8,128)S(1)} custom-call(bf16[256,768]{1,0:T(8,128)(2,1)S(1)} %collective-permute-done.14.c_first, bf16[256,768]{1,0:T(8,128)(2,1)S(1)} %collective-permute-done.15.c_second, f32[384,768]{1,0:T(8,128)S(1)} %get-tuple-element.95.x_first, f32[384,768]{1,0:T(8,128)S(1)} %get-tuple-element.96.x_second, ...), custom_call_target="tpu_custom_call" | custom-call | flops 1358954496 | bytes 9437184 | tf_op jit(solution)/shard_map/cond/branch_1_fun/early/pallas_call | solution.py:495
  45.0 0.0 collective-permute-done.10.c_first
  45.0 2.5 %collective-permute-done.11.c_second = bf16[128,768]{1,0:T(8,128)(2,1)S(1)} collective-permute-done((bf16[128,768]{1,0:T(8,128)(2,1)S(1)}, bf16[128,768]{1,0:T(8,128)(2,1)S(1)}, u32[]{:S(2)}, u32[]{:S(2)}) %collective-permute-start.11) | collective-permute-done | bytes 196640 | tf_op jit(solution)/shard_map/cond/branch_1_fun/ppermute | solution.py:369
  47.5 1.8 %late.4 = f32[1,1,2,384,384]{4,3,2,1,0:T(8,128)} custom-call(bf16[128,768]{1,0:T(8,128)(2,1)S(1)} %collective-permute-done.10.c_first, bf16[128,768]{1,0:T(8,128)(2,1)S(1)} %collective-permute-done.11.c_second, f32[384,768]{1,0:T(8,128)S(1)} %get-tuple-element.95.x_first, f32[384,768]{1,0:T(8,128)S(1)} %get-tuple-element.96.x_second, ...), custom_call_target="tpu_custom_call" | custom-call | flops 905969664 | bytes 9437184 | tf_op jit(solution)/shard_map/cond/branch_1_fun/late/pallas_call | solution.py:504
Async XLA Ops:
  0.0 2.6 %copy-start = (bf16[1,1,2,384,384]{4,3,2,1,0:T(8,128)(2,1)S(1)}, bf16[1,1,2,384,384]{4,3,2,1,0:T(8,128)(2,1)}, u32[]{:S(2)}) copy-start(bf16[1,1,2,384,384]{4,3,2,1,0:T(8,128)(2,1)} %param.11) | copy-start | bytes 1769476
  2.9 10.0 %collective-permute-start.8 = (bf16[1,1,2,384,384]{4,3,2,1,0:T(8,128)(2,1)S(1)}, bf16[1,1,2,384,384]{4,3,2,1,0:T(8,128)(2,1)S(1)}, u32[]{:S(2)}, u32[]{:S(2)}) collective-permute-start(bf16[1,1,2,384,384]{4,3,2,1,0:T(8,128)(2,1)S(1)} %get-tuple-element.88), channel_id=1, source_target_pairs={{0,1},{1,0},{2,3},{3,2},{4,5},{5,4},{6,7},{7,6},{8,9},{9,8},{10,11... | collective-permute-start | bytes 1769480 | tf_op jit(solution)/shard_map/cond/branch_1_fun/ppermute | solution.py:369
  3.0 11.2 %collective-permute-start.9 = (bf16[1,1,2,384,384]{4,3,2,1,0:T(8,128)(2,1)S(1)}, bf16[1,1,2,384,384]{4,3,2,1,0:T(8,128)(2,1)S(1)}, u32[]{:S(2)}, u32[]{:S(2)}) collective-permute-start(bf16[1,1,2,384,384]{4,3,2,1,0:T(8,128)(2,1)S(1)} %get-tuple-element.88), channel_id=1, source_target_pairs={{1,2},{2,1},{3,4},{4,3},{5,6},{6,5},{9,10},{10,9},{11,12},{12,11},... | collective-permute-start | bytes 1769480 | tf_op jit(solution)/shard_map/cond/branch_1_fun/ppermute | solution.py:369
  5.5 23.6 %collective-permute-start.12 = (bf16[608,768]{1,0:T(8,128)(2,1)S(1)}, bf16[608,768]{1,0:T(8,128)(2,1)S(1)}, u32[]{:S(2)}, u32[]{:S(2)}) collective-permute-start(bf16[608,768]{1,0:T(8,128)(2,1)S(1)} %get-tuple-element.91), channel_id=1, source_target_pairs={{0,8},{8,0},{16,24},{24,16},{32,40},{40,32},{48,56},{56,48},{64,72... | collective-permute-start | bytes 2801672 | tf_op jit(solution)/shard_map/cond/branch_1_fun/ppermute | solution.py:369
  6.4 28.8 %collective-permute-start.13 = (bf16[608,768]{1,0:T(8,128)(2,1)S(1)}, bf16[608,768]{1,0:T(8,128)(2,1)S(1)}, u32[]{:S(2)}, u32[]{:S(2)}) collective-permute-start(bf16[608,768]{1,0:T(8,128)(2,1)S(1)} %get-tuple-element.92), channel_id=1, source_target_pairs={{8,16},{16,8},{24,32},{32,24},{40,48},{48,40},{56,64},{64,56},{72,... | collective-permute-start | bytes 2801672 | tf_op jit(solution)/shard_map/cond/branch_1_fun/ppermute | solution.py:369
  14.5 23.1 %collective-permute-start.14 = (bf16[256,768]{1,0:T(8,128)(2,1)S(1)}, bf16[256,768]{1,0:T(8,128)(2,1)S(1)}, u32[]{:S(2)}, u32[]{:S(2)}) collective-permute-start(bf16[256,768]{1,0:T(8,128)(2,1)S(1)} %get-tuple-element.98.early), channel_id=1, source_target_pairs={{0,8},{8,0},{16,24},{24,16},{32,40},{40,32},{48,56},{56,48},{64,72... | collective-permute-start | bytes 1179656 | tf_op jit(solution)/shard_map/cond/branch_1_fun/ppermute | solution.py:369
  15.3 28.3 %collective-permute-start.15 = (bf16[256,768]{1,0:T(8,128)(2,1)S(1)}, bf16[256,768]{1,0:T(8,128)(2,1)S(1)}, u32[]{:S(2)}, u32[]{:S(2)}) collective-permute-start(bf16[256,768]{1,0:T(8,128)(2,1)S(1)} %get-tuple-element.98.early), channel_id=1, source_target_pairs={{8,16},{16,8},{24,32},{32,24},{40,48},{48,40},{56,64},{64,56},{72,... | collective-permute-start | bytes 1179656 | tf_op jit(solution)/shard_map/cond/branch_1_fun/ppermute | solution.py:369
  21.1 23.9 %collective-permute-start.10 = (bf16[128,768]{1,0:T(8,128)(2,1)S(1)}, bf16[128,768]{1,0:T(8,128)(2,1)S(1)}, u32[]{:S(2)}, u32[]{:S(2)}) collective-permute-start(bf16[128,768]{1,0:T(8,128)(2,1)S(1)} %get-tuple-element.89.late), channel_id=1, source_target_pairs={{0,8},{8,0},{16,24},{24,16},{32,40},{40,32},{48,56},{56,48},{64,72... | collective-permute-start | bytes 589832 | tf_op jit(solution)/shard_map/cond/branch_1_fun/ppermute | solution.py:369
  29.2 18.3 %collective-permute-start.11 = (bf16[128,768]{1,0:T(8,128)(2,1)S(1)}, bf16[128,768]{1,0:T(8,128)(2,1)S(1)}, u32[]{:S(2)}, u32[]{:S(2)}) collective-permute-start(bf16[128,768]{1,0:T(8,128)(2,1)S(1)} %get-tuple-element.89.late), channel_id=1, source_target_pairs={{8,16},{16,8},{24,32},{32,24},{40,48},{48,40},{56,64},{64,56},{72,... | collective-permute-start | bytes 589832 | tf_op jit(solution)/shard_map/cond/branch_1_fun/ppermute | solution.py:369
where the time goes:
time: 50.1 us; the launch traced here: 49.8 us
  waiting for transfers between devices  16.8 us (34%)
  starting transfers between devices  16.3 us (33%)
  Pallas kernels  15.8 us (32%)
  loops' own time  0.65 us (1%)
    ppermute x8, waiting for transfers between devices, swap(): return lax.ppermute(value, axis, swaps(first, lax.axis_size(axis)))  16.8 us
    ppermute x8, starting transfers between devices, swap(): return lax.ppermute(value, axis, swaps(first, lax.axis_size(axis)))  16.3 us
    pallas_call x1, Pallas kernels, remainder(): pl.pallas_call(own_kernel, grid=(width // STRIP,), in_specs=[*[smem()] *...  2.91 us
    pallas_call x1, Pallas kernels, remainder(): pl.pallas_call(local_kernel, out_shape=square, scratch_shapes=[pltpu.VMEM...  2.84 us
    pallas_call x1, Pallas kernels, program(): pl.pallas_call(side_kernel, in_specs=[hbm()] * 4, out_specs=[pl.BlockSpec...  2.63 us
    pallas_call x1, Pallas kernels, remainder(): pl.pallas_call(green_kernel, out_shape=[jax.ShapeDtypeStruct((3 * wide, w...  2.12 us
    pallas_call x1, Pallas kernels, remainder(): pl.pallas_call(functools.partial(arrive_kernel, reach), in_specs=[smem()]...  1.82 us
    pallas_call x1, Pallas kernels, remainder(): pl.pallas_call(late_kernel, out_specs=hbm(), out_shape=pltpu.HBM((1, 1, 2...  1.78 us
  transfers between devices with their start and end apart: 8, of which 6 were waited for; matrix products, arithmetic and copies ran while one was open for 0% of the time, Pallas kernels for 23%

commit v1 on v0

--- a/solution.py
+++ b/solution.py
@@ -110,12 +110,12 @@
     tables = [
         pltpu.make_async_copy(src, dst, table_sems.at[n]) for n, (src, dst) in enumerate(moves)
     ]
-    copies = [
-        pltpu.make_async_copy(
-            sigma.at[0, 0, :, :, pl.ds(c * height, height), :], held.at[c], sems.at[c]
-        )
-        for c in range(chunks)
-    ]
+
+    def pull(c):
+        rows = pl.ds(pl.multiple_of(c * height, height), height)
+        return pltpu.make_async_copy(sigma.at[0, 0, :, :, rows, :], held.at[c], sems.at[c])
+
+    copies = [pull(c) for c in range(chunks)]
     for copy in tables + copies:
         copy.start()
     for copy in tables:
@@ -152,8 +152,8 @@
 
     @pl.when(shared)
     def _():
-        for c in range(chunks):
-            copies[c].wait()
+        def merge_strip(c, carry):
+            pull(c).wait()
             for number, which, reaches in merges:
 
                 @pl.when(number > 1)
@@ -161,6 +161,10 @@
                     for part in range(2):
                         total = strip_sum(held.at[c], part, reaches, lanes, c)
                         held[c, which, part] = total.astype(BF16)
+
+            return carry
+
+        lax.fori_loop(0, chunks, merge_strip, 0)
 
     for index, reach in enumerate(LEVELS):
 

time: 50.1 us -> 50 us (level)
  starting transfers between devices: 16.3 us -> 17.6 us
  waiting for transfers between devices: 16.8 us -> 15.9 us
    ppermute x8, starting transfers between devices: 16.3 us -> 17.6 us  [swap(): return lax.ppermute(value, axis, swaps(first, lax.axis_size(axis)))]
    ppermute x8, waiting for transfers between devices: 16.8 us -> 15.9 us  [swap(): return lax.ppermute(value, axis, swaps(first, lax.axis_size(axis)))]
where the time goes in v1:
time: 50 us; the launch traced here: 49.7 us
  starting transfers between devices  17.6 us (35%)
  waiting for transfers between devices  15.9 us (32%)
  Pallas kernels  15.4 us (31%)
  loops' own time  0.61 us (1%)
    ppermute x8, starting transfers between devices, swap(): return lax.ppermute(value, axis, swaps(first, lax.axis_size(axis)))  17.6 us
    ppermute x8, waiting for transfers between devices, swap(): return lax.ppermute(value, axis, swaps(first, lax.axis_size(axis)))  15.9 us
    pallas_call x1, Pallas kernels, remainder(): pl.pallas_call(own_kernel, grid=(width // STRIP,), in_specs=[*[smem()] *...  2.91 us
    pallas_call x1, Pallas kernels, remainder(): pl.pallas_call(local_kernel, out_shape=square, scratch_shapes=[pltpu.VMEM...  2.84 us
    pallas_call x1, Pallas kernels, program(): pl.pallas_call(side_kernel, in_specs=[hbm()] * 4, out_specs=[pl.BlockSpec...  2.28 us
    pallas_call x1, Pallas kernels, remainder(): pl.pallas_call(green_kernel, out_shape=[jax.ShapeDtypeStruct((3 * wide, w...  2.12 us
    pallas_call x1, Pallas kernels, remainder(): pl.pallas_call(functools.partial(arrive_kernel, reach), in_specs=[smem()]...  1.82 us
    pallas_call x1, Pallas kernels, remainder(): pl.pallas_call(late_kernel, out_specs=hbm(), out_shape=pltpu.HBM((1, 1, 2...  1.78 us
  transfers between devices with their start and end apart: 8, of which 6 were waited for; matrix products, arithmetic and copies ran while one was open for 0% of the time, Pallas kernels for 23%

profile of v1, /device:TPU:130, one launch (start us, length us, event | category | flops | bytes accessed | tf_op | source)
XLA Modules:
  0.0 49.7 jit_solution(10146666403675912586)
XLA Ops:
  0.0 0.0 copy-start
  0.0 2.3 %side.1 = (bf16[480,768]{1,0:T(8,128)(2,1)S(1)}, bf16[480,768]{1,0:T(8,128)(2,1)S(1)}, bf16[608,768]{1,0:T(8,128)(2,1)S(1)}, bf16[608,768]{1,0:T(8,128)(2,1)S(1)...) custom-call(s32[3,32]{1,0:T(4,128)} %bitcast.4, ...), custom_call_target="tpu_custom_call" | custom-call | flops 3000000000 | bytes 4128768 | tf_op jit(solution)/shard_map/side/pallas_call | solution.py:392
  2.3 0.0 copy-done
  2.3 47.2 %conditional.1 = (f32[1,1,2,384,384]{4,3,2,1,0:T(8,128)}) conditional(s32[]{:T(128)} %bitcast.3, (s32[3,32]{1,0:T(4,128)}, s32[1,32]{1,0:T(1,128)}, s32[3,32]{1,0:T(4,128)}, bf16[1,1,3,2,384,384]{5,4,3,2,1,0:T(8,128)(2,1)}, bf16[1,1,2,384,384]{4,3,2,1,0:T(8,128)(2,1)S(1)}, /*index=5*/bf16[480,768]{1,0:T(8,128)(2,1)S(1)}, ...), branch_computations={%region_0.0_spmd, %region_1.0_spmd, %region_2.0_spmd} | conditional | flops 13888802816 | bytes 70779208 | solution.py:413
  2.3 0.1 collective-permute-start.8
  2.4 2.5 %collective-permute-start.9 = (bf16[1,1,2,384,384]{4,3,2,1,0:T(8,128)(2,1)S(1)}, bf16[1,1,2,384,384]{4,3,2,1,0:T(8,128)(2,1)S(1)}, u32[]{:S(2)}, u32[]{:S(2)}) collective-permute-start(bf16[1,1,2,384,384]{4,3,2,1,0:T(8,128)(2,1)S(1)} %get-tuple-element.88), channel_id=1, source_target_pairs={{1,2},{2,1},{3,4},{4,3},{5,6},{6,5},{9,10},{10,9},{11,12},{12,11},... | collective-permute-start | bytes 1769480 | tf_op jit(solution)/shard_map/cond/branch_1_fun/ppermute | solution.py:373
  5.0 1.2 %collective-permute-start.12 = (bf16[608,768]{1,0:T(8,128)(2,1)S(1)}, bf16[608,768]{1,0:T(8,128)(2,1)S(1)}, u32[]{:S(2)}, u32[]{:S(2)}) collective-permute-start(bf16[608,768]{1,0:T(8,128)(2,1)S(1)} %get-tuple-element.91), channel_id=1, source_target_pairs={{0,8},{8,0},{16,24},{24,16},{32,40},{40,32},{48,56},{56,48},{64,72... | collective-permute-start | bytes 2801672 | tf_op jit(solution)/shard_map/cond/branch_1_fun/ppermute | solution.py:373
  6.1 3.9 %collective-permute-start.13 = (bf16[608,768]{1,0:T(8,128)(2,1)S(1)}, bf16[608,768]{1,0:T(8,128)(2,1)S(1)}, u32[]{:S(2)}, u32[]{:S(2)}) collective-permute-start(bf16[608,768]{1,0:T(8,128)(2,1)S(1)} %get-tuple-element.92), channel_id=1, source_target_pairs={{8,16},{16,8},{24,32},{32,24},{40,48},{48,40},{56,64},{64,56},{72,... | collective-permute-start | bytes 2801672 | tf_op jit(solution)/shard_map/cond/branch_1_fun/ppermute | solution.py:373
  10.0 2.9 %own.4 = (bf16[384,768]{1,0:T(8,128)(2,1)S(1)}, bf16[384,768]{1,0:T(8,128)(2,1)S(1)}, f32[384,768]{1,0:T(8,128)S(1)}) custom-call(s32[3,32]{1,0:T(4,128)} %get-tuple-element.83.off, s32[1,32]{1,0:T(1,128)} %get-tuple-element.84.cnt, s32[3,32]{1,0:T(4,128)} %get-tuple-element.85.rng, bf16[1,1,3,2,384,384]{5,4,3,2,1,0:T(8,128)(2,1)} %get-tuple-element.86.sigma), custom_call_target="tpu_custom_call" | custom-call | flops 3000000000 | bytes 4128768 | tf_op jit(solution)/shard_map/cond/branch_1_fun/own/pallas_call | solution.py:429
  12.9 0.0 collective-permute-done.8.one
  12.9 0.7 %collective-permute-done.9.two = bf16[1,1,2,384,384]{4,3,2,1,0:T(8,128)(2,1)S(1)} collective-permute-done((bf16[1,1,2,384,384]{4,3,2,1,0:T(8,128)(2,1)S(1)}, bf16[1,1,2,384,384]{4,3,2,1,0:T(8,128)(2,1)S(1)}, u32[]{:S(2)}, u32[]{:S(2)}) %collective-permute-start.9) | collective-permute-done | bytes 589856 | tf_op jit(solution)/shard_map/cond/branch_1_fun/ppermute | solution.py:373
  13.6 0.3 centre.4
  13.9 1.2 %collective-permute-start.14 = (bf16[256,768]{1,0:T(8,128)(2,1)S(1)}, bf16[256,768]{1,0:T(8,128)(2,1)S(1)}, u32[]{:S(2)}, u32[]{:S(2)}) collective-permute-start(bf16[256,768]{1,0:T(8,128)(2,1)S(1)} %get-tuple-element.98.early), channel_id=1, source_target_pairs={{0,8},{8,0},{16,24},{24,16},{32,40},{40,32},{48,56},{56,48},{64,72... | collective-permute-start | bytes 1179656 | tf_op jit(solution)/shard_map/cond/branch_1_fun/ppermute | solution.py:373
  15.1 3.8 %collective-permute-start.15 = (bf16[256,768]{1,0:T(8,128)(2,1)S(1)}, bf16[256,768]{1,0:T(8,128)(2,1)S(1)}, u32[]{:S(2)}, u32[]{:S(2)}) collective-permute-start(bf16[256,768]{1,0:T(8,128)(2,1)S(1)} %get-tuple-element.98.early), channel_id=1, source_target_pairs={{8,16},{16,8},{24,32},{32,24},{40,48},{48,40},{56,64},{64,56},{72,... | collective-permute-start | bytes 1179656 | tf_op jit(solution)/shard_map/cond/branch_1_fun/ppermute | solution.py:373
  18.9 2.1 %green.4 = (bf16[2304,768]{1,0:T(8,128)(2,1)S(1)}, bf16[384,768]{1,0:T(8,128)(2,1)S(1)}, bf16[384,1024]{1,0:T(8,128)(2,1)S(1)}, bf16[384,512]{1,0:T(8,128)(2,1)S(1)}) custom-call(bf16[1,1,3,2,384,384]{5,4,3,2,1,0:T(8,128)(2,1)} %get-tuple-element.93.green), custom_call_target="tpu_custom_call" | custom-call | flops 4000000000 | bytes 7077888 | tf_op jit(solution)/shard_map/cond/branch_1_fun/green/pallas_call | solution.py:462
  21.0 1.1 %collective-permute-start.10 = (bf16[128,768]{1,0:T(8,128)(2,1)S(1)}, bf16[128,768]{1,0:T(8,128)(2,1)S(1)}, u32[]{:S(2)}, u32[]{:S(2)}) collective-permute-start(bf16[128,768]{1,0:T(8,128)(2,1)S(1)} %get-tuple-element.89.late), channel_id=1, source_target_pairs={{0,8},{8,0},{16,24},{24,16},{32,40},{40,32},{48,56},{56,48},{64,72... | collective-permute-start | bytes 589832 | tf_op jit(solution)/shard_map/cond/branch_1_fun/ppermute | solution.py:373
  22.1 2.8 %local.4.partial = f32[384,768]{1,0:T(8,128)S(1)} custom-call(bf16[384,768]{1,0:T(8,128)(2,1)S(1)} %get-tuple-element.100.near_first, bf16[256,768]{1,0:T(8,128)(2,1)S(1)} %get-tuple-element.98.early, bf16[128,768]{1,0:T(8,128)(2,1)S(1)} %get-tuple-element.89.late, bf16[384,768]{1,0:T(8,128)(2,1)S(1)} %get-tuple-element.101.near_second, ...), custom_call_target="tpu_custom_call" | custom-call | flops 1811939328 | bytes 9437184 | tf_op jit(solution)/shard_map/cond/branch_1_fun/local/pallas_call | solution.py:477
  24.9 3.7 %collective-permute-done.12.from_first = bf16[608,768]{1,0:T(8,128)(2,1)S(1)} collective-permute-done((bf16[608,768]{1,0:T(8,128)(2,1)S(1)}, bf16[608,768]{1,0:T(8,128)(2,1)S(1)}, u32[]{:S(2)}, u32[]{:S(2)}) %collective-permute-start.12) | collective-permute-done | bytes 933920 | tf_op jit(solution)/shard_map/cond/branch_1_fun/ppermute | solution.py:373
  28.6 4.0 %collective-permute-start.11 = (bf16[128,768]{1,0:T(8,128)(2,1)S(1)}, bf16[128,768]{1,0:T(8,128)(2,1)S(1)}, u32[]{:S(2)}, u32[]{:S(2)}) collective-permute-start(bf16[128,768]{1,0:T(8,128)(2,1)S(1)} %get-tuple-element.89.late), channel_id=1, source_target_pairs={{8,16},{16,8},{24,32},{32,24},{40,48},{48,40},{56,64},{64,56},{72,... | collective-permute-start | bytes 589832 | tf_op jit(solution)/shard_map/cond/branch_1_fun/ppermute | solution.py:373
  32.6 2.3 %collective-permute-done.13.from_second = bf16[608,768]{1,0:T(8,128)(2,1)S(1)} collective-permute-done((bf16[608,768]{1,0:T(8,128)(2,1)S(1)}, bf16[608,768]{1,0:T(8,128)(2,1)S(1)}, u32[]{:S(2)}, u32[]{:S(2)}) %collective-permute-start.13) | collective-permute-done | bytes 933920 | tf_op jit(solution)/shard_map/cond/branch_1_fun/ppermute | solution.py:373
  34.9 1.8 %arrive.4 = (f32[384,768]{1,0:T(8,128)S(1)}, f32[384,768]{1,0:T(8,128)S(1)}) custom-call(s32[2]{0:T(128)S(4)} %get-tuple-element.90.roles, bf16[608,768]{1,0:T(8,128)(2,1)S(1)} %collective-permute-done.12.from_first, bf16[608,768]{1,0:T(8,128)(2,1)S(1)} %collective-permute-done.13.from_second, bf16[2304,768]{1,0:T(8,128)(2,1)S(1)} %get-tuple-element.94.right), custom_call_target="tpu_custom_call" | custom-call | flops 1811939328 | bytes 9437184 | tf_op jit(solution)/shard_map/cond/branch_1_fun/arrive/pallas_call | solution.py:489
  36.7 0.3 collective-permute-done.14.c_first
  37.0 6.3 %collective-permute-done.15.c_second = bf16[256,768]{1,0:T(8,128)(2,1)S(1)} collective-permute-done((bf16[256,768]{1,0:T(8,128)(2,1)S(1)}, bf16[256,768]{1,0:T(8,128)(2,1)S(1)}, u32[]{:S(2)}, u32[]{:S(2)}) %collective-permute-start.15) | collective-permute-done | bytes 393248 | tf_op jit(solution)/shard_map/cond/branch_1_fun/ppermute | solution.py:373
  43.3 1.4 %early.4.partial = f32[384,768]{1,0:T(8,128)S(1)} custom-call(bf16[256,768]{1,0:T(8,128)(2,1)S(1)} %collective-permute-done.14.c_first, bf16[256,768]{1,0:T(8,128)(2,1)S(1)} %collective-permute-done.15.c_second, f32[384,768]{1,0:T(8,128)S(1)} %get-tuple-element.95.x_first, f32[384,768]{1,0:T(8,128)S(1)} %get-tuple-element.96.x_second, ...), custom_call_target="tpu_custom_call" | custom-call | flops 1358954496 | bytes 9437184 | tf_op jit(solution)/shard_map/cond/branch_1_fun/early/pallas_call | solution.py:499
  44.7 0.0 collective-permute-done.10.c_first
  44.8 2.5 %collective-permute-done.11.c_second = bf16[128,768]{1,0:T(8,128)(2,1)S(1)} collective-permute-done((bf16[128,768]{1,0:T(8,128)(2,1)S(1)}, bf16[128,768]{1,0:T(8,128)(2,1)S(1)}, u32[]{:S(2)}, u32[]{:S(2)}) %collective-permute-start.11) | collective-permute-done | bytes 196640 | tf_op jit(solution)/shard_map/cond/branch_1_fun/ppermute | solution.py:373
  47.3 1.8 %late.4 = f32[1,1,2,384,384]{4,3,2,1,0:T(8,128)} custom-call(bf16[128,768]{1,0:T(8,128)(2,1)S(1)} %collective-permute-done.10.c_first, bf16[128,768]{1,0:T(8,128)(2,1)S(1)} %collective-permute-done.11.c_second, f32[384,768]{1,0:T(8,128)S(1)} %get-tuple-element.95.x_first, f32[384,768]{1,0:T(8,128)S(1)} %get-tuple-element.96.x_second, ...), custom_call_target="tpu_custom_call" | custom-call | flops 905969664 | bytes 9437184 | tf_op jit(solution)/shard_map/cond/branch_1_fun/late/pallas_call | solution.py:508
Async XLA Ops:
  0.0 2.3 %copy-start = (bf16[1,1,2,384,384]{4,3,2,1,0:T(8,128)(2,1)S(1)}, bf16[1,1,2,384,384]{4,3,2,1,0:T(8,128)(2,1)}, u32[]{:S(2)}) copy-start(bf16[1,1,2,384,384]{4,3,2,1,0:T(8,128)(2,1)} %param.11) | copy-start | bytes 1769476
  2.3 10.6 %collective-permute-start.8 = (bf16[1,1,2,384,384]{4,3,2,1,0:T(8,128)(2,1)S(1)}, bf16[1,1,2,384,384]{4,3,2,1,0:T(8,128)(2,1)S(1)}, u32[]{:S(2)}, u32[]{:S(2)}) collective-permute-start(bf16[1,1,2,384,384]{4,3,2,1,0:T(8,128)(2,1)S(1)} %get-tuple-element.88), channel_id=1, source_target_pairs={{0,1},{1,0},{2,3},{3,2},{4,5},{5,4},{6,7},{7,6},{8,9},{9,8},{10,11... | collective-permute-start | bytes 1769480 | tf_op jit(solution)/shard_map/cond/branch_1_fun/ppermute | solution.py:373
  2.4 11.2 %collective-permute-start.9 = (bf16[1,1,2,384,384]{4,3,2,1,0:T(8,128)(2,1)S(1)}, bf16[1,1,2,384,384]{4,3,2,1,0:T(8,128)(2,1)S(1)}, u32[]{:S(2)}, u32[]{:S(2)}) collective-permute-start(bf16[1,1,2,384,384]{4,3,2,1,0:T(8,128)(2,1)S(1)} %get-tuple-element.88), channel_id=1, source_target_pairs={{1,2},{2,1},{3,4},{4,3},{5,6},{6,5},{9,10},{10,9},{11,12},{12,11},... | collective-permute-start | bytes 1769480 | tf_op jit(solution)/shard_map/cond/branch_1_fun/ppermute | solution.py:373
  5.0 23.6 %collective-permute-start.12 = (bf16[608,768]{1,0:T(8,128)(2,1)S(1)}, bf16[608,768]{1,0:T(8,128)(2,1)S(1)}, u32[]{:S(2)}, u32[]{:S(2)}) collective-permute-start(bf16[608,768]{1,0:T(8,128)(2,1)S(1)} %get-tuple-element.91), channel_id=1, source_target_pairs={{0,8},{8,0},{16,24},{24,16},{32,40},{40,32},{48,56},{56,48},{64,72... | collective-permute-start | bytes 2801672 | tf_op jit(solution)/shard_map/cond/branch_1_fun/ppermute | solution.py:373
  6.1 28.8 %collective-permute-start.13 = (bf16[608,768]{1,0:T(8,128)(2,1)S(1)}, bf16[608,768]{1,0:T(8,128)(2,1)S(1)}, u32[]{:S(2)}, u32[]{:S(2)}) collective-permute-start(bf16[608,768]{1,0:T(8,128)(2,1)S(1)} %get-tuple-element.92), channel_id=1, source_target_pairs={{8,16},{16,8},{24,32},{32,24},{40,48},{48,40},{56,64},{64,56},{72,... | collective-permute-start | bytes 2801672 | tf_op jit(solution)/shard_map/cond/branch_1_fun/ppermute | solution.py:373
  13.9 23.1 %collective-permute-start.14 = (bf16[256,768]{1,0:T(8,128)(2,1)S(1)}, bf16[256,768]{1,0:T(8,128)(2,1)S(1)}, u32[]{:S(2)}, u32[]{:S(2)}) collective-permute-start(bf16[256,768]{1,0:T(8,128)(2,1)S(1)} %get-tuple-element.98.early), channel_id=1, source_target_pairs={{0,8},{8,0},{16,24},{24,16},{32,40},{40,32},{48,56},{56,48},{64,72... | collective-permute-start | bytes 1179656 | tf_op jit(solution)/shard_map/cond/branch_1_fun/ppermute | solution.py:373
  15.1 28.3 %collective-permute-start.15 = (bf16[256,768]{1,0:T(8,128)(2,1)S(1)}, bf16[256,768]{1,0:T(8,128)(2,1)S(1)}, u32[]{:S(2)}, u32[]{:S(2)}) collective-permute-start(bf16[256,768]{1,0:T(8,128)(2,1)S(1)} %get-tuple-element.98.early), channel_id=1, source_target_pairs={{8,16},{16,8},{24,32},{32,24},{40,48},{48,40},{56,64},{64,56},{72,... | collective-permute-start | bytes 1179656 | tf_op jit(solution)/shard_map/cond/branch_1_fun/ppermute | solution.py:373
  21.0 23.7 %collective-permute-start.10 = (bf16[128,768]{1,0:T(8,128)(2,1)S(1)}, bf16[128,768]{1,0:T(8,128)(2,1)S(1)}, u32[]{:S(2)}, u32[]{:S(2)}) collective-permute-start(bf16[128,768]{1,0:T(8,128)(2,1)S(1)} %get-tuple-element.89.late), channel_id=1, source_target_pairs={{0,8},{8,0},{16,24},{24,16},{32,40},{40,32},{48,56},{56,48},{64,72... | collective-permute-start | bytes 589832 | tf_op jit(solution)/shard_map/cond/branch_1_fun/ppermute | solution.py:373
  28.6 18.7 %collective-permute-start.11 = (bf16[128,768]{1,0:T(8,128)(2,1)S(1)}, bf16[128,768]{1,0:T(8,128)(2,1)S(1)}, u32[]{:S(2)}, u32[]{:S(2)}) collective-permute-start(bf16[128,768]{1,0:T(8,128)(2,1)S(1)} %get-tuple-element.89.late), channel_id=1, source_target_pairs={{8,16},{16,8},{24,32},{32,24},{40,48},{48,40},{56,64},{64,56},{72,... | collective-permute-start | bytes 589832 | tf_op jit(solution)/shard_map/cond/branch_1_fun/ppermute | solution.py:373

commit v2 on v1

--- a/solution.py
+++ b/solution.py
@@ -236,23 +236,27 @@
 def green_kernel(green, right, left, left_early, left_late):
     width = green.shape[-1]
     s = toward()
-    for slot, o in enumerate((1 + s, 1, 1 - s)):
-        real, imag = green[0, 0, o, 0], green[0, 0, o, 1]
-        real_t, imag_t = real.T, imag.T
-        at = 2 * slot * width
-        right[at : at + width, :width] = real_t
-        right[at : at + width, width:] = -imag_t
-        right[at + width : at + 2 * width, :width] = imag_t
-        right[at + width : at + 2 * width, width:] = real_t
-        if slot == 1:
-            left[:, :width] = real
-            left[:, width:] = imag
-        else:
-            for out, first, last in ((left_early, 0, SPLIT), (left_late, SPLIT, width)):
-                height = last - first
-                to = slot * height
-                out[:, to : to + height] = real[:, first:last]
-                out[:, to + height : to + 2 * height] = imag[:, first:last]
+
+    def turn(slot, carry):
+        o = 1 + s * (1 - slot)
+        real_t, imag_t = green[0, 0, o, 0].T, green[0, 0, o, 1].T
+        above = pl.ds(pl.multiple_of(2 * slot * width, width), width)
+        below = pl.ds(pl.multiple_of((2 * slot + 1) * width, width), width)
+        right[above, :width] = real_t
+        right[above, width:] = -imag_t
+        right[below, :width] = imag_t
+        right[below, width:] = real_t
+        return carry
+
+    lax.fori_loop(0, 3, turn, 0)
+    left[:, :width] = green[0, 0, 1, 0]
+    left[:, width:] = green[0, 0, 1, 1]
+    for out, first, last in ((left_early, 0, SPLIT), (left_late, SPLIT, width)):
+        height = last - first
+        for n, o in enumerate((1 + s, 1 - s)):
+            for part in range(2):
+                to = (2 * n + part) * height
+                out[:, to : to + height] = green[0, 0, o, part, :, first:last]
 
 
 def spread(x, out, first):

time: 50 us -> 50 us (level)
  transfers between devices with their start and end apart: 8 -> 8, of which waited for: 6 -> 6; matrix products, arithmetic and copies ran while one was open for 0% -> 0% of each run, Pallas kernels for 23% -> 24%
where the time goes in v2:
time: 50 us; the launch traced here: 49.7 us
  starting transfers between devices  17.6 us (35%)
  Pallas kernels  15.8 us (32%)
  waiting for transfers between devices  15.5 us (31%)
  loops' own time  0.61 us (1%)
    ppermute x8, starting transfers between devices, swap(): return lax.ppermute(value, axis, swaps(first, lax.axis_size(axis)))  17.6 us
    ppermute x8, waiting for transfers between devices, swap(): return lax.ppermute(value, axis, swaps(first, lax.axis_size(axis)))  15.5 us
    pallas_call x1, Pallas kernels, remainder(): pl.pallas_call(own_kernel, grid=(width // STRIP,), in_specs=[*[smem()] *...  2.91 us
    pallas_call x1, Pallas kernels, remainder(): pl.pallas_call(local_kernel, out_shape=square, scratch_shapes=[pltpu.VMEM...  2.84 us
    pallas_call x1, Pallas kernels, remainder(): pl.pallas_call(green_kernel, out_shape=[jax.ShapeDtypeStruct((3 * wide, w...  2.46 us
    pallas_call x1, Pallas kernels, program(): pl.pallas_call(side_kernel, in_specs=[hbm()] * 4, out_specs=[pl.BlockSpec...  2.28 us
    pallas_call x1, Pallas kernels, remainder(): pl.pallas_call(functools.partial(arrive_kernel, reach), in_specs=[smem()]...  1.82 us
    pallas_call x1, Pallas kernels, remainder(): pl.pallas_call(late_kernel, out_specs=hbm(), out_shape=pltpu.HBM((1, 1, 2...  1.78 us
  transfers between devices with their start and end apart: 8, of which 6 were waited for; matrix products, arithmetic and copies ran while one was open for 0% of the time, Pallas kernels for 24%

profile of v2, /device:TPU:130, one launch (start us, length us, event | category | flops | bytes accessed | tf_op | source)
XLA Modules:
  0.0 49.7 jit_solution(18196769300328145245)
XLA Ops:
  0.0 0.0 copy-start
  0.0 2.3 %side.1 = (bf16[480,768]{1,0:T(8,128)(2,1)S(1)}, bf16[480,768]{1,0:T(8,128)(2,1)S(1)}, bf16[608,768]{1,0:T(8,128)(2,1)S(1)}, bf16[608,768]{1,0:T(8,128)(2,1)S(1)...) custom-call(s32[3,32]{1,0:T(4,128)} %bitcast.4, ...), custom_call_target="tpu_custom_call" | custom-call | flops 3000000000 | bytes 4128768 | tf_op jit(solution)/shard_map/side/pallas_call | solution.py:396
  2.3 0.0 copy-done
  2.3 47.2 %conditional.1 = (f32[1,1,2,384,384]{4,3,2,1,0:T(8,128)}) conditional(s32[]{:T(128)} %bitcast.3, (s32[3,32]{1,0:T(4,128)}, s32[1,32]{1,0:T(1,128)}, s32[3,32]{1,0:T(4,128)}, bf16[1,1,3,2,384,384]{5,4,3,2,1,0:T(8,128)(2,1)}, bf16[1,1,2,384,384]{4,3,2,1,0:T(8,128)(2,1)S(1)}, /*index=5*/bf16[480,768]{1,0:T(8,128)(2,1)S(1)}, ...), branch_computations={%region_0.0_spmd, %region_1.0_spmd, %region_2.0_spmd} | conditional | flops 13888802816 | bytes 70779208 | solution.py:417
  2.3 0.1 collective-permute-start.8
  2.4 2.5 %collective-permute-start.9 = (bf16[1,1,2,384,384]{4,3,2,1,0:T(8,128)(2,1)S(1)}, bf16[1,1,2,384,384]{4,3,2,1,0:T(8,128)(2,1)S(1)}, u32[]{:S(2)}, u32[]{:S(2)}) collective-permute-start(bf16[1,1,2,384,384]{4,3,2,1,0:T(8,128)(2,1)S(1)} %get-tuple-element.88), channel_id=1, source_target_pairs={{1,2},{2,1},{3,4},{4,3},{5,6},{6,5},{9,10},{10,9},{11,12},{12,11},... | collective-permute-start | bytes 1769480 | tf_op jit(solution)/shard_map/cond/branch_1_fun/ppermute | solution.py:377
  5.0 1.2 %collective-permute-start.12 = (bf16[608,768]{1,0:T(8,128)(2,1)S(1)}, bf16[608,768]{1,0:T(8,128)(2,1)S(1)}, u32[]{:S(2)}, u32[]{:S(2)}) collective-permute-start(bf16[608,768]{1,0:T(8,128)(2,1)S(1)} %get-tuple-element.91), channel_id=1, source_target_pairs={{0,8},{8,0},{16,24},{24,16},{32,40},{40,32},{48,56},{56,48},{64,72... | collective-permute-start | bytes 2801672 | tf_op jit(solution)/shard_map/cond/branch_1_fun/ppermute | solution.py:377
  6.1 3.6 %collective-permute-start.13 = (bf16[608,768]{1,0:T(8,128)(2,1)S(1)}, bf16[608,768]{1,0:T(8,128)(2,1)S(1)}, u32[]{:S(2)}, u32[]{:S(2)}) collective-permute-start(bf16[608,768]{1,0:T(8,128)(2,1)S(1)} %get-tuple-element.92), channel_id=1, source_target_pairs={{8,16},{16,8},{24,32},{32,24},{40,48},{48,40},{56,64},{64,56},{72,... | collective-permute-start | bytes 2801672 | tf_op jit(solution)/shard_map/cond/branch_1_fun/ppermute | solution.py:377
  9.8 2.9 %own.4 = (bf16[384,768]{1,0:T(8,128)(2,1)S(1)}, bf16[384,768]{1,0:T(8,128)(2,1)S(1)}, f32[384,768]{1,0:T(8,128)S(1)}) custom-call(s32[3,32]{1,0:T(4,128)} %get-tuple-element.83.off, s32[1,32]{1,0:T(1,128)} %get-tuple-element.84.cnt, s32[3,32]{1,0:T(4,128)} %get-tuple-element.85.rng, bf16[1,1,3,2,384,384]{5,4,3,2,1,0:T(8,128)(2,1)} %get-tuple-element.86.sigma), custom_call_target="tpu_custom_call" | custom-call | flops 3000000000 | bytes 4128768 | tf_op jit(solution)/shard_map/cond/branch_1_fun/own/pallas_call | solution.py:433
  12.7 0.0 collective-permute-done.8.one
  12.7 0.9 %collective-permute-done.9.two = bf16[1,1,2,384,384]{4,3,2,1,0:T(8,128)(2,1)S(1)} collective-permute-done((bf16[1,1,2,384,384]{4,3,2,1,0:T(8,128)(2,1)S(1)}, bf16[1,1,2,384,384]{4,3,2,1,0:T(8,128)(2,1)S(1)}, u32[]{:S(2)}, u32[]{:S(2)}) %collective-permute-start.9) | collective-permute-done | bytes 589856 | tf_op jit(solution)/shard_map/cond/branch_1_fun/ppermute | solution.py:377
  13.6 0.3 centre.4
  13.9 1.4 %collective-permute-start.14 = (bf16[256,768]{1,0:T(8,128)(2,1)S(1)}, bf16[256,768]{1,0:T(8,128)(2,1)S(1)}, u32[]{:S(2)}, u32[]{:S(2)}) collective-permute-start(bf16[256,768]{1,0:T(8,128)(2,1)S(1)} %get-tuple-element.98.early), channel_id=1, source_target_pairs={{0,8},{8,0},{16,24},{24,16},{32,40},{40,32},{48,56},{56,48},{64,72... | collective-permute-start | bytes 1179656 | tf_op jit(solution)/shard_map/cond/branch_1_fun/ppermute | solution.py:377
  15.3 3.6 %collective-permute-start.15 = (bf16[256,768]{1,0:T(8,128)(2,1)S(1)}, bf16[256,768]{1,0:T(8,128)(2,1)S(1)}, u32[]{:S(2)}, u32[]{:S(2)}) collective-permute-start(bf16[256,768]{1,0:T(8,128)(2,1)S(1)} %get-tuple-element.98.early), channel_id=1, source_target_pairs={{8,16},{16,8},{24,32},{32,24},{40,48},{48,40},{56,64},{64,56},{72,... | collective-permute-start | bytes 1179656 | tf_op jit(solution)/shard_map/cond/branch_1_fun/ppermute | solution.py:377
  18.9 2.5 %green.4 = (bf16[2304,768]{1,0:T(8,128)(2,1)S(1)}, bf16[384,768]{1,0:T(8,128)(2,1)S(1)}, bf16[384,1024]{1,0:T(8,128)(2,1)S(1)}, bf16[384,512]{1,0:T(8,128)(2,1)S(1)}) custom-call(bf16[1,1,3,2,384,384]{5,4,3,2,1,0:T(8,128)(2,1)} %get-tuple-element.93.green), custom_call_target="tpu_custom_call" | custom-call | flops 4000000000 | bytes 7077888 | tf_op jit(solution)/shard_map/cond/branch_1_fun/green/pallas_call | solution.py:466
  21.4 1.2 %collective-permute-start.10 = (bf16[128,768]{1,0:T(8,128)(2,1)S(1)}, bf16[128,768]{1,0:T(8,128)(2,1)S(1)}, u32[]{:S(2)}, u32[]{:S(2)}) collective-permute-start(bf16[128,768]{1,0:T(8,128)(2,1)S(1)} %get-tuple-element.89.late), channel_id=1, source_target_pairs={{0,8},{8,0},{16,24},{24,16},{32,40},{40,32},{48,56},{56,48},{64,72... | collective-permute-start | bytes 589832 | tf_op jit(solution)/shard_map/cond/branch_1_fun/ppermute | solution.py:377
  22.6 2.8 %local.4.partial = f32[384,768]{1,0:T(8,128)S(1)} custom-call(bf16[384,768]{1,0:T(8,128)(2,1)S(1)} %get-tuple-element.100.near_first, bf16[256,768]{1,0:T(8,128)(2,1)S(1)} %get-tuple-element.98.early, bf16[128,768]{1,0:T(8,128)(2,1)S(1)} %get-tuple-element.89.late, bf16[384,768]{1,0:T(8,128)(2,1)S(1)} %get-tuple-element.101.near_second, ...), custom_call_target="tpu_custom_call" | custom-call | flops 1811939328 | bytes 9437184 | tf_op jit(solution)/shard_map/cond/branch_1_fun/local/pallas_call | solution.py:481
  25.5 3.1 %collective-permute-done.12.from_first = bf16[608,768]{1,0:T(8,128)(2,1)S(1)} collective-permute-done((bf16[608,768]{1,0:T(8,128)(2,1)S(1)}, bf16[608,768]{1,0:T(8,128)(2,1)S(1)}, u32[]{:S(2)}, u32[]{:S(2)}) %collective-permute-start.12) | collective-permute-done | bytes 933920 | tf_op jit(solution)/shard_map/cond/branch_1_fun/ppermute | solution.py:377
  28.6 4.0 %collective-permute-start.11 = (bf16[128,768]{1,0:T(8,128)(2,1)S(1)}, bf16[128,768]{1,0:T(8,128)(2,1)S(1)}, u32[]{:S(2)}, u32[]{:S(2)}) collective-permute-start(bf16[128,768]{1,0:T(8,128)(2,1)S(1)} %get-tuple-element.89.late), channel_id=1, source_target_pairs={{8,16},{16,8},{24,32},{32,24},{40,48},{48,40},{56,64},{64,56},{72,... | collective-permute-start | bytes 589832 | tf_op jit(solution)/shard_map/cond/branch_1_fun/ppermute | solution.py:377
  32.6 2.3 %collective-permute-done.13.from_second = bf16[608,768]{1,0:T(8,128)(2,1)S(1)} collective-permute-done((bf16[608,768]{1,0:T(8,128)(2,1)S(1)}, bf16[608,768]{1,0:T(8,128)(2,1)S(1)}, u32[]{:S(2)}, u32[]{:S(2)}) %collective-permute-start.13) | collective-permute-done | bytes 933920 | tf_op jit(solution)/shard_map/cond/branch_1_fun/ppermute | solution.py:377
  34.9 1.8 %arrive.4 = (f32[384,768]{1,0:T(8,128)S(1)}, f32[384,768]{1,0:T(8,128)S(1)}) custom-call(s32[2]{0:T(128)S(4)} %get-tuple-element.90.roles, bf16[608,768]{1,0:T(8,128)(2,1)S(1)} %collective-permute-done.12.from_first, bf16[608,768]{1,0:T(8,128)(2,1)S(1)} %collective-permute-done.13.from_second, bf16[2304,768]{1,0:T(8,128)(2,1)S(1)} %get-tuple-element.94.right), custom_call_target="tpu_custom_call" | custom-call | flops 1811939328 | bytes 9437184 | tf_op jit(solution)/shard_map/cond/branch_1_fun/arrive/pallas_call | solution.py:493
  36.7 0.3 collective-permute-done.14.c_first
  37.0 6.3 %collective-permute-done.15.c_second = bf16[256,768]{1,0:T(8,128)(2,1)S(1)} collective-permute-done((bf16[256,768]{1,0:T(8,128)(2,1)S(1)}, bf16[256,768]{1,0:T(8,128)(2,1)S(1)}, u32[]{:S(2)}, u32[]{:S(2)}) %collective-permute-start.15) | collective-permute-done | bytes 393248 | tf_op jit(solution)/shard_map/cond/branch_1_fun/ppermute | solution.py:377
  43.3 1.4 %early.4.partial = f32[384,768]{1,0:T(8,128)S(1)} custom-call(bf16[256,768]{1,0:T(8,128)(2,1)S(1)} %collective-permute-done.14.c_first, bf16[256,768]{1,0:T(8,128)(2,1)S(1)} %collective-permute-done.15.c_second, f32[384,768]{1,0:T(8,128)S(1)} %get-tuple-element.95.x_first, f32[384,768]{1,0:T(8,128)S(1)} %get-tuple-element.96.x_second, ...), custom_call_target="tpu_custom_call" | custom-call | flops 1358954496 | bytes 9437184 | tf_op jit(solution)/shard_map/cond/branch_1_fun/early/pallas_call | solution.py:503
  44.7 0.0 collective-permute-done.10.c_first
  44.8 2.5 %collective-permute-done.11.c_second = bf16[128,768]{1,0:T(8,128)(2,1)S(1)} collective-permute-done((bf16[128,768]{1,0:T(8,128)(2,1)S(1)}, bf16[128,768]{1,0:T(8,128)(2,1)S(1)}, u32[]{:S(2)}, u32[]{:S(2)}) %collective-permute-start.11) | collective-permute-done | bytes 196640 | tf_op jit(solution)/shard_map/cond/branch_1_fun/ppermute | solution.py:377
  47.3 1.8 %late.4 = f32[1,1,2,384,384]{4,3,2,1,0:T(8,128)} custom-call(bf16[128,768]{1,0:T(8,128)(2,1)S(1)} %collective-permute-done.10.c_first, bf16[128,768]{1,0:T(8,128)(2,1)S(1)} %collective-permute-done.11.c_second, f32[384,768]{1,0:T(8,128)S(1)} %get-tuple-element.95.x_first, f32[384,768]{1,0:T(8,128)S(1)} %get-tuple-element.96.x_second, ...), custom_call_target="tpu_custom_call" | custom-call | flops 905969664 | bytes 9437184 | tf_op jit(solution)/shard_map/cond/branch_1_fun/late/pallas_call | solution.py:512
Async XLA Ops:
  0.0 2.3 %copy-start = (bf16[1,1,2,384,384]{4,3,2,1,0:T(8,128)(2,1)S(1)}, bf16[1,1,2,384,384]{4,3,2,1,0:T(8,128)(2,1)}, u32[]{:S(2)}) copy-start(bf16[1,1,2,384,384]{4,3,2,1,0:T(8,128)(2,1)} %param.11) | copy-start | bytes 1769476
  2.3 10.4 %collective-permute-start.8 = (bf16[1,1,2,384,384]{4,3,2,1,0:T(8,128)(2,1)S(1)}, bf16[1,1,2,384,384]{4,3,2,1,0:T(8,128)(2,1)S(1)}, u32[]{:S(2)}, u32[]{:S(2)}) collective-permute-start(bf16[1,1,2,384,384]{4,3,2,1,0:T(8,128)(2,1)S(1)} %get-tuple-element.88), channel_id=1, source_target_pairs={{0,1},{1,0},{2,3},{3,2},{4,5},{5,4},{6,7},{7,6},{8,9},{9,8},{10,11... | collective-permute-start | bytes 1769480 | tf_op jit(solution)/shard_map/cond/branch_1_fun/ppermute | solution.py:377
  2.4 11.2 %collective-permute-start.9 = (bf16[1,1,2,384,384]{4,3,2,1,0:T(8,128)(2,1)S(1)}, bf16[1,1,2,384,384]{4,3,2,1,0:T(8,128)(2,1)S(1)}, u32[]{:S(2)}, u32[]{:S(2)}) collective-permute-start(bf16[1,1,2,384,384]{4,3,2,1,0:T(8,128)(2,1)S(1)} %get-tuple-element.88), channel_id=1, source_target_pairs={{1,2},{2,1},{3,4},{4,3},{5,6},{6,5},{9,10},{10,9},{11,12},{12,11},... | collective-permute-start | bytes 1769480 | tf_op jit(solution)/shard_map/cond/branch_1_fun/ppermute | solution.py:377
  5.0 23.6 %collective-permute-start.12 = (bf16[608,768]{1,0:T(8,128)(2,1)S(1)}, bf16[608,768]{1,0:T(8,128)(2,1)S(1)}, u32[]{:S(2)}, u32[]{:S(2)}) collective-permute-start(bf16[608,768]{1,0:T(8,128)(2,1)S(1)} %get-tuple-element.91), channel_id=1, source_target_pairs={{0,8},{8,0},{16,24},{24,16},{32,40},{40,32},{48,56},{56,48},{64,72... | collective-permute-start | bytes 2801672 | tf_op jit(solution)/shard_map/cond/branch_1_fun/ppermute | solution.py:377
  6.1 28.8 %collective-permute-start.13 = (bf16[608,768]{1,0:T(8,128)(2,1)S(1)}, bf16[608,768]{1,0:T(8,128)(2,1)S(1)}, u32[]{:S(2)}, u32[]{:S(2)}) collective-permute-start(bf16[608,768]{1,0:T(8,128)(2,1)S(1)} %get-tuple-element.92), channel_id=1, source_target_pairs={{8,16},{16,8},{24,32},{32,24},{40,48},{48,40},{56,64},{64,56},{72,... | collective-permute-start | bytes 2801672 | tf_op jit(solution)/shard_map/cond/branch_1_fun/ppermute | solution.py:377
  13.9 23.1 %collective-permute-start.14 = (bf16[256,768]{1,0:T(8,128)(2,1)S(1)}, bf16[256,768]{1,0:T(8,128)(2,1)S(1)}, u32[]{:S(2)}, u32[]{:S(2)}) collective-permute-start(bf16[256,768]{1,0:T(8,128)(2,1)S(1)} %get-tuple-element.98.early), channel_id=1, source_target_pairs={{0,8},{8,0},{16,24},{24,16},{32,40},{40,32},{48,56},{56,48},{64,72... | collective-permute-start | bytes 1179656 | tf_op jit(solution)/shard_map/cond/branch_1_fun/ppermute | solution.py:377
  15.3 28.0 %collective-permute-start.15 = (bf16[256,768]{1,0:T(8,128)(2,1)S(1)}, bf16[256,768]{1,0:T(8,128)(2,1)S(1)}, u32[]{:S(2)}, u32[]{:S(2)}) collective-permute-start(bf16[256,768]{1,0:T(8,128)(2,1)S(1)} %get-tuple-element.98.early), channel_id=1, source_target_pairs={{8,16},{16,8},{24,32},{32,24},{40,48},{48,40},{56,64},{64,56},{72,... | collective-permute-start | bytes 1179656 | tf_op jit(solution)/shard_map/cond/branch_1_fun/ppermute | solution.py:377
  21.4 23.3 %collective-permute-start.10 = (bf16[128,768]{1,0:T(8,128)(2,1)S(1)}, bf16[128,768]{1,0:T(8,128)(2,1)S(1)}, u32[]{:S(2)}, u32[]{:S(2)}) collective-permute-start(bf16[128,768]{1,0:T(8,128)(2,1)S(1)} %get-tuple-element.89.late), channel_id=1, source_target_pairs={{0,8},{8,0},{16,24},{24,16},{32,40},{40,32},{48,56},{56,48},{64,72... | collective-permute-start | bytes 589832 | tf_op jit(solution)/shard_map/cond/branch_1_fun/ppermute | solution.py:377
  28.6 18.7 %collective-permute-start.11 = (bf16[128,768]{1,0:T(8,128)(2,1)S(1)}, bf16[128,768]{1,0:T(8,128)(2,1)S(1)}, u32[]{:S(2)}, u32[]{:S(2)}) collective-permute-start(bf16[128,768]{1,0:T(8,128)(2,1)S(1)} %get-tuple-element.89.late), channel_id=1, source_target_pairs={{8,16},{16,8},{24,32},{32,24},{40,48},{48,40},{56,64},{64,56},{72,... | collective-permute-start | bytes 589832 | tf_op jit(solution)/shard_map/cond/branch_1_fun/ppermute | solution.py:377
